TPU v7x, 32 devices: a whole 2x2x4 slice. The times are simulated.
32 devices in a mesh: band: 4 (over y, core), tile: 8 (over z, x).
Axes of the slice: x: 2, y: 2, z: 4, core: 2. Of those that a mesh axis runs over, the one named last changes fastest.
Arguments:
- patches: bfloat16 [262144, 128], P(('band', 'tile')), may hold values from -6 to 6
- pair_patch: int32 [4096], P(('band', 'tile')), may hold values from 0 to 63
- pair_atm: int32 [4096], P(('band', 'tile')), may hold values from 0 to 4095, as said below
- numerators: int32 [4096, 128, 32], P(('band', 'tile')), may hold values from 0 to 16777215
- counts: int32 [32], P(('band', 'tile')), may hold values from 32 to 128, as said below
Outputs:
- atmosphere: float32 [131072, 128], P(('band', 'tile'))
Inputs may be any that keep to these rules, and one draw needn't show every extreme that they name: Block pair_atm[g] is owned by device pair_atm[g] // 128 (band-major device order). Every live pair of device (b, t) targets an owner in band b (any tile) or one of (b - 1, t), (b + 1, t). Among one device's live pairs at most 32 target one owner and at most 16 distinct blocks of one owner; both are reached on some device in every draw. Slots that are not live hold arbitrary blocks in range. `counts`: the value 128 occurs on some device in every draw.
All inputs are finite; a program needn't handle non-finite values.
Results may differ from a plain program's by a relative error of at most 0.0026.
Values sent between devices are 32-bit elements; how exact they have to be, the bound alone decides.
No kernel may reach another device: no remote copies, remote signals or barrier semaphores. Data moves between devices by JAX's collectives and lax.ppermute only.
A program may use at most 64 MiB of HBM per device.

v0:
```python
import jax
import jax.numpy as jnp
from jax import lax
from jax.sharding import PartitionSpec as P

CELLS_DEV = 4096


SCALE = 2.0 ** (-27)


def shifted(value, axis, steps):
    count = lax.axis_size(axis)
    first, last = (max(0, -steps), min(count, count - steps))
    return lax.ppermute(value, axis, [(source, source + steps) for source in range(first, last)])


def slot_ranks(owners, blocks_local, live_pairs):
    position = jnp.arange(owners.shape[0])
    earlier = position[None, :] < position[:, None]
    both_live = live_pairs[None, :] & live_pairs[:, None]
    same_owner = (owners[:, None] == owners[None, :]) & both_live
    same_block = same_owner & (blocks_local[:, None] == blocks_local[None, :])
    leading = jnp.logical_not(jnp.any(same_block & earlier, axis=1))
    leader_rank = jnp.sum((same_owner & earlier & leading[None, :]).astype(jnp.int32), axis=1)
    first_match = same_block & leading[None, :]
    return jnp.sum(jnp.where(first_match, leader_rank[None, :], 0), axis=1)


def pack(flattened, rows_index, selected, blocks_local, rows_total):
    onehot = (rows_index[None, :] == jnp.arange(rows_total)[:, None]) & selected[None, :]
    payload = jnp.dot(onehot.astype(jnp.float32), flattened, precision=lax.Precision.HIGHEST)
    labels = jnp.max(jnp.where(onehot, blocks_local[None, :], -1), axis=1)
    return (payload, labels)


def unpack(payload, labels, blocks_owned):
    onehot = (labels[None, :] == jnp.arange(blocks_owned)[:, None]).astype(jnp.float32)
    return jnp.dot(onehot, payload, precision=lax.Precision.HIGHEST)


def along_band(parcel, offset_by):
    return shifted((parcel[0], parcel[1]), "band", offset_by)


def per_device(patches, pair_patch, pair_atm, numerators, counts):
    pairs_here, patch_rows, cell_rows = numerators.shape
    flux_width = patches.shape[1]
    blocks_owned = CELLS_DEV // cell_rows
    capacity = pairs_here // 4
    grouped = patches.reshape(-1, patch_rows, flux_width)
    live_pairs = jnp.arange(pairs_here) < counts[0]
    weight = (numerators.astype(jnp.float32) * SCALE).astype(jnp.bfloat16)
    chosen = grouped[pair_patch]
    partial_value = jnp.einsum("jpa,jpf->jaf", weight, chosen, preferred_element_type=jnp.float32)
    flattened = partial_value.reshape(pairs_here, cell_rows * flux_width)
    owners = pair_atm // blocks_owned
    blocks_local = pair_atm % blocks_owned
    slot_rank = slot_ranks(owners, blocks_local, live_pairs)
    bucket_size = capacity // 2
    tile_count = lax.axis_size("tile")
    band_now = lax.axis_index("band")
    tile_now = lax.axis_index("tile")
    owner_band = owners // tile_count
    owner_tile = owners % tile_count
    in_band = live_pairs & (owner_band == band_now)
    rows_index = jnp.where(in_band, owner_tile * bucket_size + slot_rank, -1)
    payload, labels = pack(flattened, rows_index, in_band, blocks_local, tile_count * bucket_size)

    def bucket(target):
        addressed = live_pairs & (owners == target)
        target_rows = jnp.where(addressed, slot_rank, -1)
        return pack(flattened, target_rows, addressed, blocks_local, bucket_size)

    upper_index = (band_now + 1) * tile_count + tile_now
    lower_index = (band_now - 1) * tile_count + tile_now
    from_below = along_band(bucket(upper_index), 1)
    from_above = along_band(bucket(lower_index), -1)
    band_payload = jnp.concatenate([from_below[0], from_above[0]], axis=0)
    band_labels = jnp.concatenate([from_below[1], from_above[1]], axis=0)
    payload, labels = (
        lax.all_to_all(
            payload.reshape(tile_count, bucket_size, -1),
            "tile",
            split_axis=0,
            concat_axis=0,
            tiled=True,
        ),
        lax.all_to_all(
            labels.reshape(tile_count, bucket_size), "tile", split_axis=0, concat_axis=0, tiled=True
        ),
    )
    payload = jnp.concatenate([payload.reshape(tile_count * bucket_size, -1), band_payload], axis=0)
    labels = jnp.concatenate([labels.reshape(-1), band_labels], axis=0)
    summed = unpack(payload, labels, blocks_owned)
    return summed.reshape(blocks_owned * cell_rows, flux_width)


def solution(mesh):
    placed = (
        P(("band", "tile"), None),
        P(("band", "tile")),
        P(("band", "tile")),
        P(("band", "tile"), None, None),
        P(("band", "tile")),
    )
    return jax.shard_map(
        per_device, mesh=mesh, in_specs=placed, out_specs=P(("band", "tile"), None), check_vma=False
    )
```

profile of v0, /device:TPU:0, one launch (start us, length us, event | category | flops | bytes accessed | tf_op | source)
XLA Modules:
  0.0 86.8 jit_solution(12213925503748507290)
XLA Ops:
  0.0 0.0 copy-start
  0.0 0.8 and_select_fusion
  1.5 0.2 fusion.17
  1.7 0.2 convert_reduce_fusion
  1.9 0.2 select_reduce_fusion.1
  2.1 0.1 select_reduce_fusion
  2.2 0.7 all_to_all.9
  2.9 7.3 %all-to-all-start = ((s32[8,1,16]{2,1,0:T(1,128)}), s32[8,1,16]{2,1,0:T(1,128)S(1)}, u32[]{:S(2)}, u32[]{:S(2)}) async-start(s32[8,1,16]{2,1,0:T(1,128)} %bitcast.1), calls=%async_computation | async-start | bytes 8192 | tf_op jit(solution)/shard_map/all_to_all | solution.py:89
  10.2 0.7 compare_select_fusion
  10.9 0.0 copy-done
  10.9 3.0 %gather_fusion = bf16[128,128,128]{2,1,0:T(8,128)(2,1)} fusion(bf16[64,128,128]{2,1,0:T(8,128)(2,1)S(1)} %bitcast.14, s32[1024]{0:T(1024)S(1)} %pad_clamp_fusion), kind=kCustom, calls=%fused_computation | custom fusion | bytes 8389120 | tf_op jit(solution)/shard_map/gather | solution.py:54
  13.9 5.3 %fusion.12 = f32[128,32,128]{2,1,0:T(8,128)} fusion(bf16[128,128,128]{2,1,0:T(8,128)(2,1)} %gather_fusion, s32[128,128,32]{1,2,0:T(8,128)} %param.8), kind=kOutput, calls=%fused_computation.14 | convolution fusion | flops 135790592 | bytes 8388608 | tf_op jit(solution)/shard_map/jpa,jpf->jaf/dot_general | solution.py:55
  19.2 2.7 %reshape.80 = f32[128,4096,1]{1,0,2:T(8,128)} reshape(f32[128,32,128]{2,1,0:T(8,128)} %fusion.12) | data formatting | bytes 4194304 | tf_op jit(solution)/shard_map/reshape | solution.py:56
  21.9 4.1 %fusion.20 = f32[8,16,4096]{2,1,0:T(8,128)} fusion(f32[128,4096,1]{1,0,2:T(8,128)} %reshape.80, s32[8,16]{1,0:T(8,128)S(1)} %multiply_add_fusion, s32[128]{0:T(128)S(1)} %get-tuple-element.7, pred[128]{0:T(512)(128)(4,1)S(1)} %get-tuple-element.8), kind=kOutput, calls=%fused_computation.28 | convolution fusion | flops 805339136 | bytes 4195456 | tf_op jit(solution)/shard_map/dot_general | solution.py:32
  26.1 0.0 all-to-all-done
  26.1 6.0 %all-to-all-start.1 = ((f32[8,16,4096]{2,1,0:T(8,128)}), f32[8,16,4096]{2,1,0:T(8,128)}, u32[]{:S(2)}, u32[]{:S(2)}) async-start(f32[8,16,4096]{2,1,0:T(8,128)} %fusion.20), calls=%async_computation.1 | async-start | bytes 4194304 | tf_op jit(solution)/shard_map/all_to_all | solution.py:82
  32.1 0.0 copy-start.1
  32.1 3.6 %fusion.8 = f32[16,4096]{1,0:T(8,128)S(1)} fusion(f32[16,8,32,128]{3,2,1,0:T(8,128)} %bitcast.15, s32[128]{0:T(128)S(1)} %get-tuple-element.13, pred[128]{0:T(512)(128)(4,1)S(1)} %get-tuple-element.14), kind=kOutput, calls=%fused_computation.9 | convolution fusion | flops 100667392 | bytes 2359936 | tf_op jit(solution)/shard_map/dot_general | solution.py:32
  35.7 1.3 %collective-permute-start.3 = (f32[16,4096]{1,0:T(8,128)S(1)}, f32[16,4096]{1,0:T(8,128)S(1)}, u32[]{:S(2)}, u32[]{:S(2)}) collective-permute-start(f32[16,4096]{1,0:T(8,128)S(1)} %fusion.8), channel_id=1, source_target_pairs={{8,0},{16,8},{24,16},{9,1},{17,9},{25,17},{10,2},{18,10},{26,18},{... | collective-permute-start | bytes 786440 | tf_op jit(solution)/shard_map/ppermute | solution.py:15
  37.0 0.0 copy-done.1
  37.0 2.0 %fusion.6 = f32[16,4096]{1,0:T(8,128)S(1)} fusion(f32[16,8,32,128]{3,2,1,0:T(8,128)S(1)} %bitcast.16, s32[128]{0:T(128)S(1)} %get-tuple-element.15, pred[128]{0:T(512)(128)(4,1)S(1)} %get-tuple-element.16), kind=kOutput, calls=%fused_computation.7 | convolution fusion | flops 100667392 | bytes 2359936 | tf_op jit(solution)/shard_map/dot_general | solution.py:32
  39.0 3.0 %collective-permute-start.2 = (f32[16,4096]{1,0:T(8,128)S(1)}, f32[16,4096]{1,0:T(8,128)S(1)}, u32[]{:S(2)}, u32[]{:S(2)}) collective-permute-start(f32[16,4096]{1,0:T(8,128)S(1)} %fusion.6), channel_id=1, source_target_pairs={{0,8},{8,16},{16,24},{1,9},{9,17},{17,25},{2,10},{10,18},{18,26},{... | collective-permute-start | bytes 786440 | tf_op jit(solution)/shard_map/ppermute | solution.py:15
  42.0 0.1 select_reduce_fusion.3
  42.1 1.3 %collective-permute-start.1 = (s32[16]{0:T(128)S(1)}, s32[16]{0:T(128)S(1)}, u32[]{:S(2)}, u32[]{:S(2)}) collective-permute-start(s32[16]{0:T(128)S(1)} %get-tuple-element.6), channel_id=1, source_target_pairs={{8,0},{16,8},{24,16},{9,1},{17,9},{25,17},{10,2},{18,10},{26,18},{... | collective-permute-start | bytes 200 | tf_op jit(solution)/shard_map/ppermute | solution.py:15
  43.4 3.7 %collective-permute-start = (s32[16]{0:T(128)S(1)}, s32[16]{0:T(128)S(1)}, u32[]{:S(2)}, u32[]{:S(2)}) collective-permute-start(s32[16]{0:T(128)S(1)} %get-tuple-element.5), channel_id=1, source_target_pairs={{0,8},{8,16},{16,24},{1,9},{9,17},{17,25},{2,10},{10,18},{18,26},{... | collective-permute-start | bytes 200 | tf_op jit(solution)/shard_map/ppermute | solution.py:15
  47.1 0.5 broadcast.108
  47.6 0.7 reduce.3
  48.3 0.1 reshape.66
  48.4 0.0 collective-permute-done.1
  48.4 0.0 collective-permute-done
  48.4 0.1 pad_add_fusion
  48.5 0.0 collective-permute-done.3
  48.5 0.0 collective-permute-done.2
  48.5 31.4 %all-to-all-done.1 = f32[8,16,4096]{2,1,0:T(8,128)} async-done(((f32[8,16,4096]{2,1,0:T(8,128)}), f32[8,16,4096]{2,1,0:T(8,128)}, u32[]{:S(2)}, u32[]{:S(2)}) %all-to-all-start.1) | async-done | bytes 2097184 | tf_op jit(solution)/shard_map/all_to_all | solution.py:82
  79.9 4.3 %fusion = f32[128,4096]{1,0:T(8,128)} fusion(f32[16,4096]{1,0:T(8,128)S(1)} %collective-permute-done.3, f32[16,4096]{1,0:T(8,128)S(1)} %collective-permute-done.2, f32[128,4096]{1,0:T(8,128)} %bitcast.3, s32[160]{0:T(256)S(1)} %pad_add_fusion), kind=kOutput, calls=%fused_computation.1 | convolution fusion | flops 1007964160 | bytes 4719232 | tf_op jit(solution)/shard_map/dot_general | solution.py:39
  84.1 2.7 %reshape.70 = f32[4096,128]{1,0:T(8,128)} reshape(f32[128,4096]{1,0:T(8,128)} %fusion) | data formatting | bytes 4194304 | tf_op jit(solution)/shard_map/reshape | solution.py:96
  (5 shorter events, 0.0 us)
Async XLA Ops:
  0.0 10.9 %copy-start = (bf16[8192,128]{1,0:T(8,128)(2,1)S(1)}, bf16[8192,128]{1,0:T(8,128)(2,1)}, u32[]{:S(2)}) copy-start(bf16[8192,128]{1,0:T(8,128)(2,1)} %param.5) | copy-start | bytes 6291460
  2.9 23.2 %all-to-all-start = ((s32[8,1,16]{2,1,0:T(1,128)}), s32[8,1,16]{2,1,0:T(1,128)S(1)}, u32[]{:S(2)}, u32[]{:S(2)}) async-start(s32[8,1,16]{2,1,0:T(1,128)} %bitcast.1), calls=%async_computation | async-start | bytes 8192 | tf_op jit(solution)/shard_map/all_to_all | solution.py:89
  26.1 53.8 %all-to-all-start.1 = ((f32[8,16,4096]{2,1,0:T(8,128)}), f32[8,16,4096]{2,1,0:T(8,128)}, u32[]{:S(2)}, u32[]{:S(2)}) async-start(f32[8,16,4096]{2,1,0:T(8,128)} %fusion.20), calls=%async_computation.1 | async-start | bytes 4194304 | tf_op jit(solution)/shard_map/all_to_all | solution.py:82
  32.1 4.9 %copy-start.1 = (f32[128,32,128]{2,1,0:T(8,128)S(1)}, f32[128,32,128]{2,1,0:T(8,128)}, u32[]{:S(2)}) copy-start(f32[128,32,128]{2,1,0:T(8,128)} %fusion.12) | copy-start | bytes 6291460
  35.7 12.8 %collective-permute-start.3 = (f32[16,4096]{1,0:T(8,128)S(1)}, f32[16,4096]{1,0:T(8,128)S(1)}, u32[]{:S(2)}, u32[]{:S(2)}) collective-permute-start(f32[16,4096]{1,0:T(8,128)S(1)} %fusion.8), channel_id=1, source_target_pairs={{8,0},{16,8},{24,16},{9,1},{17,9},{25,17},{10,2},{18,10},{26,18},{... | collective-permute-start | bytes 786440 | tf_op jit(solution)/shard_map/ppermute | solution.py:15
  39.0 9.5 %collective-permute-start.2 = (f32[16,4096]{1,0:T(8,128)S(1)}, f32[16,4096]{1,0:T(8,128)S(1)}, u32[]{:S(2)}, u32[]{:S(2)}) collective-permute-start(f32[16,4096]{1,0:T(8,128)S(1)} %fusion.6), channel_id=1, source_target_pairs={{0,8},{8,16},{16,24},{1,9},{9,17},{17,25},{2,10},{10,18},{18,26},{... | collective-permute-start | bytes 786440 | tf_op jit(solution)/shard_map/ppermute | solution.py:15
  42.1 6.2 %collective-permute-start.1 = (s32[16]{0:T(128)S(1)}, s32[16]{0:T(128)S(1)}, u32[]{:S(2)}, u32[]{:S(2)}) collective-permute-start(s32[16]{0:T(128)S(1)} %get-tuple-element.6), channel_id=1, source_target_pairs={{8,0},{16,8},{24,16},{9,1},{17,9},{25,17},{10,2},{18,10},{26,18},{... | collective-permute-start | bytes 200 | tf_op jit(solution)/shard_map/ppermute | solution.py:15
  43.4 4.9 %collective-permute-start = (s32[16]{0:T(128)S(1)}, s32[16]{0:T(128)S(1)}, u32[]{:S(2)}, u32[]{:S(2)}) collective-permute-start(s32[16]{0:T(128)S(1)} %get-tuple-element.5), channel_id=1, source_target_pairs={{0,8},{8,16},{16,24},{1,9},{9,17},{17,25},{2,10},{10,18},{18,26},{... | collective-permute-start | bytes 200 | tf_op jit(solution)/shard_map/ppermute | solution.py:15
where the time goes:
time: 87.3 us; the launch traced here: 86.8 us
  waiting for transfers between devices  31.4 us (36%)
  starting transfers between devices  22.6 us (26%)
  matrix products  19.3 us (22%)
  local copies, waits for them, and re-layouts  9.71 us (11%)
  other arithmetic  3.08 us (4%)
    all_to_all x1, waiting for transfers between devices, per_device(): lax.all_to_all(payload.reshape(tile_count, bucket_size, -1), 'tile', spli...  31.4 us
    dot_general x3, matrix products, pack(): jnp.dot(onehot.astype(jnp.float32), flattened, precision=lax.Precision.HI...  9.69 us
    ppermute x4, starting transfers between devices, shifted(): lax.ppermute(value, axis, [(source, source + steps) for source in range(f...  9.29 us
    all_to_all x1, starting transfers between devices, per_device(): lax.all_to_all(labels.reshape(tile_count, bucket_size), 'tile', split_axi...  7.28 us
    all_to_all x1, starting transfers between devices, per_device(): lax.all_to_all(payload.reshape(tile_count, bucket_size, -1), 'tile', spli...  5.99 us
    dot_general x1, matrix products, per_device(): jnp.einsum('jpa,jpf->jaf', weight, chosen, preferred_element_type=jnp.flo...  5.35 us
    dot_general x1, matrix products, unpack(): return jnp.dot(onehot, payload, precision=lax.Precision.HIGHEST)  4.28 us
    gather x1, local copies, waits for them, and re-layouts, per_device(): chosen = grouped[pair_patch]  3.01 us
  transfers between devices with their start and end apart: 6, of which 1 were waited for; matrix products, arithmetic and copies ran while one was open for 26% of the time, Pallas kernels for 0%

commit v1 on v0

v1 whole, which is shorter than its diff:
```python
import functools

import jax
import jax.numpy as jnp
from jax import lax
from jax.experimental import pallas as pl
from jax.experimental.pallas import tpu as pltpu
from jax.sharding import PartitionSpec as P

CELLS_DEV = 4096


SCALE = 2.0 ** (-27)
LABEL_ROWS = 8
UNROLL = 16


def shifted(value, axis, steps):
    count = lax.axis_size(axis)
    first, last = (max(0, -steps), min(count, count - steps))
    return lax.ppermute(value, axis, [(source, source + steps) for source in range(first, last)])


def pack_kernel(
    tile_count, blocks_owned, slots,
    place_ref, count_ref, patch_ref, atm_ref, empty_ref, patches_hbm, numer_hbm,
    tile_out, upper_out, lower_out,
    buckets, patches, numer, table, used, row_of, patch_sem, numer_sem, table_sem, out_sem,
):
    pairs_here, cell_rows, patch_rows = numer.shape
    chunks = pairs_here // UNROLL
    bucket_rows = slots * cell_rows + LABEL_ROWS
    table_copy = pltpu.make_async_copy(empty_ref, table, table_sem)
    table_copy.start()
    patch_copy = pltpu.make_async_copy(patches_hbm, patches, patch_sem)
    patch_copy.start()

    def numer_copy(chunk):
        part = pl.ds(pl.multiple_of(chunk * UNROLL, UNROLL), UNROLL)
        return pltpu.make_async_copy(numer_hbm.at[part], numer.at[part], numer_sem.at[chunk])

    for chunk in range(chunks):
        numer_copy(chunk).start()

    count = count_ref[0]
    band_now, tile_now = place_ref[0], place_ref[1]
    del tile_now

    def clear(step, carry):
        rows = pl.ds(pl.multiple_of(step * cell_rows, cell_rows), cell_rows)
        for bucket in range(tile_count + 2):
            buckets[bucket, rows, :] = jnp.zeros((cell_rows, buckets.shape[2]), jnp.float32)
        return carry

    lax.fori_loop(0, slots, clear, 0)
    for bucket in range(tile_count + 2):
        buckets[bucket, pl.ds(slots * cell_rows, LABEL_ROWS), :] = jnp.zeros(
            (LABEL_ROWS, buckets.shape[2]), jnp.float32
        )
        used[bucket] = 0
    used[tile_count + 2] = 0
    table_copy.wait()
    lane = lax.broadcasted_iota(jnp.int32, (1, buckets.shape[2]), 1)

    def place(step, carry):
        for inner in range(4):
            pair = step * 4 + inner
            live = pair < count
            atm = atm_ref[pair]
            owner = lax.div(atm, blocks_owned)
            block = atm - owner * blocks_owned
            owner_band = lax.div(owner, tile_count)
            owner_tile = owner - owner_band * tile_count
            beyond = jnp.where(owner_band > band_now, tile_count, tile_count + 1)
            bucket = jnp.where(owner_band == band_now, owner_tile, beyond)
            bucket = jnp.where(live, bucket, tile_count + 2)
            key = bucket * blocks_owned + block
            known = table[key]
            fresh = known < 0
            slot = jnp.where(fresh, used[bucket], known)
            slot = jnp.where(live, slot, 0)
            table[key] = slot
            used[bucket] = used[bucket] + jnp.where(fresh, 1, 0)
            row_of[pair] = bucket * bucket_rows + slot * cell_rows
            row = pl.ds(slots * cell_rows, 1)
            label = (block + 1).astype(jnp.float32)
            buckets[bucket, row, :] = jnp.where(lane == slot, label, buckets[bucket, row, :])
        return carry

    lax.fori_loop(0, pairs_here // 4, place, 0)
    patch_copy.wait()
    flat = buckets.reshape(buckets.shape[0] * bucket_rows, buckets.shape[2])

    def multiply(chunk, carry):
        numer_copy(chunk).wait()
        results = []
        for inner in range(UNROLL):
            pair = chunk * UNROLL + inner
            weight = (numer[pair].astype(jnp.float32) * SCALE).astype(jnp.bfloat16)
            start = pl.multiple_of(patch_ref[pair] * patch_rows, patch_rows)
            source = patches[pl.ds(start, patch_rows), :]
            results.append(jnp.dot(weight, source, preferred_element_type=jnp.float32))
        for inner in range(UNROLL):
            rows = pl.ds(pl.multiple_of(row_of[chunk * UNROLL + inner], 8), cell_rows)
            flat[rows, :] = flat[rows, :] + results[inner]
        return carry

    busy = lax.div(count + UNROLL - 1, UNROLL)
    lax.fori_loop(0, busy, multiply, 0)

    def drain(chunk, carry):
        numer_copy(chunk).wait()
        return carry

    lax.fori_loop(busy, chunks, drain, 0)
    copies = (
        pltpu.make_async_copy(buckets.at[pl.ds(0, tile_count)], tile_out, out_sem.at[0]),
        pltpu.make_async_copy(buckets.at[tile_count], upper_out, out_sem.at[1]),
        pltpu.make_async_copy(buckets.at[tile_count + 1], lower_out, out_sem.at[2]),
    )
    for copy in copies:
        copy.start()
    for copy in copies:
        copy.wait()


def pack(place, counts, pair_patch, pair_atm, patches, numer, tile_count, blocks_owned, slots):
    pairs_here, cell_rows, patch_rows = numer.shape
    flux_width = patches.shape[1]
    bucket_rows = slots * cell_rows + LABEL_ROWS
    keys = (tile_count + 3) * blocks_owned
    empty = jnp.full((keys,), -1, jnp.int32)
    smem, hbm = pl.BlockSpec(memory_space=pltpu.SMEM), pl.BlockSpec(memory_space=pl.ANY)
    bucket = jax.ShapeDtypeStruct((bucket_rows, flux_width), jnp.float32)
    return pl.pallas_call(
        functools.partial(pack_kernel, tile_count, blocks_owned, slots),
        out_shape=(
            jax.ShapeDtypeStruct((tile_count, bucket_rows, flux_width), jnp.float32), bucket, bucket,
        ),
        in_specs=[smem, smem, smem, smem, hbm, hbm, hbm],
        out_specs=(hbm, hbm, hbm),
        scratch_shapes=[
            pltpu.VMEM((tile_count + 3, bucket_rows, flux_width), jnp.float32),
            pltpu.VMEM(patches.shape, patches.dtype),
            pltpu.VMEM(numer.shape, numer.dtype),
            pltpu.SMEM((keys,), jnp.int32),
            pltpu.SMEM((tile_count + 3,), jnp.int32),
            pltpu.SMEM((pairs_here,), jnp.int32),
            pltpu.SemaphoreType.DMA,
            pltpu.SemaphoreType.DMA((pairs_here // UNROLL,)),
            pltpu.SemaphoreType.DMA,
            pltpu.SemaphoreType.DMA((3,)),
        ],
        name="pack",
    )(place, counts, pair_patch, pair_atm, empty, patches, numer)


def unpack_kernel(
    slots, cell_rows,
    tile_hbm, below_hbm, above_hbm, out_hbm,
    total, buckets, label_rows, labels, in_sem, label_sem, out_sem,
):
    tile_count = tile_hbm.shape[0]
    copies = [
        pltpu.make_async_copy(tile_hbm.at[bucket], buckets.at[bucket], in_sem.at[bucket])
        for bucket in range(tile_count)
    ]
    copies.append(pltpu.make_async_copy(below_hbm, buckets.at[tile_count], in_sem.at[tile_count]))
    copies.append(
        pltpu.make_async_copy(above_hbm, buckets.at[tile_count + 1], in_sem.at[tile_count + 1])
    )
    for copy in copies:
        copy.start()

    def clear(step, carry):
        rows = pl.ds(pl.multiple_of(step * 128, 128), 128)
        total[rows, :] = jnp.zeros((128, total.shape[1]), jnp.float32)
        return carry

    lax.fori_loop(0, total.shape[0] // 128, clear, 0)
    for copy in copies:
        copy.wait()
    for bucket in range(tile_count + 2):
        row = buckets[bucket, pl.ds(slots * cell_rows, 1), :]
        label_rows[pl.ds(bucket, 1), :] = row.astype(jnp.int32) - 1
    label_copy = pltpu.make_async_copy(label_rows, labels, label_sem)
    label_copy.start()
    label_copy.wait()

    def add(bucket, carry):
        for slot in range(slots):
            label = labels[bucket, slot]

            @pl.when(label >= 0)
            def _():
                rows = pl.ds(pl.multiple_of(label * cell_rows, cell_rows), cell_rows)
                total[rows, :] = total[rows, :] + buckets[bucket, pl.ds(slot * cell_rows, cell_rows), :]

        return carry

    lax.fori_loop(0, tile_count + 2, add, 0)
    out_copy = pltpu.make_async_copy(total, out_hbm, out_sem)
    out_copy.start()
    out_copy.wait()


def unpack(tile_in, below, above, blocks_owned, cell_rows, slots):
    tile_count, bucket_rows, flux_width = tile_in.shape
    hbm = pl.BlockSpec(memory_space=pl.ANY)
    total = (blocks_owned * cell_rows, flux_width)
    label_shape = (-(-(tile_count + 2) // 8) * 8, flux_width)
    return pl.pallas_call(
        functools.partial(unpack_kernel, slots, cell_rows),
        out_shape=jax.ShapeDtypeStruct(total, jnp.float32),
        in_specs=[hbm, hbm, hbm],
        out_specs=hbm,
        scratch_shapes=[
            pltpu.VMEM(total, jnp.float32),
            pltpu.VMEM((tile_count + 2, bucket_rows, flux_width), jnp.float32),
            pltpu.VMEM(label_shape, jnp.int32),
            pltpu.SMEM(label_shape, jnp.int32),
            pltpu.SemaphoreType.DMA((tile_count + 2,)),
            pltpu.SemaphoreType.DMA,
            pltpu.SemaphoreType.DMA,
        ],
        name="unpack",
    )(tile_in, below, above)


def per_device(patches, pair_patch, pair_atm, numerators, counts):
    pairs_here, patch_rows, cell_rows = numerators.shape
    blocks_owned = CELLS_DEV // cell_rows
    slots = pairs_here // 8
    tile_count = lax.axis_size("tile")
    place = jnp.stack([lax.axis_index("band"), lax.axis_index("tile")]).astype(jnp.int32)
    numer = jnp.swapaxes(numerators, 1, 2)
    tiles, upper, lower = pack(
        place, counts, pair_patch, pair_atm, patches, numer, tile_count, blocks_owned, slots
    )
    tiles = lax.all_to_all(tiles, "tile", split_axis=0, concat_axis=0, tiled=True)
    below = shifted(upper, "band", 1)
    above = shifted(lower, "band", -1)
    return unpack(tiles, below, above, blocks_owned, cell_rows, slots)


def solution(mesh):
    placed = (
        P(("band", "tile"), None),
        P(("band", "tile")),
        P(("band", "tile")),
        P(("band", "tile"), None, None),
        P(("band", "tile")),
    )
    return jax.shard_map(
        per_device, mesh=mesh, in_specs=placed, out_specs=P(("band", "tile"), None), check_vma=False
    )
```

time: 87.3 us -> 71.4 us (0.82)
  matrix products: 19.3 us -> 0 us
  waiting for transfers between devices: 31.4 us -> 46.1 us
  starting transfers between devices: 22.6 us -> 9.68 us
  Pallas kernels: 0 us -> 11.8 us
  local copies, waits for them, and re-layouts: 9.71 us -> 1.95 us
  other arithmetic: 3.08 us -> 0.58 us
    dot_general x5 -> x0, matrix products: 19.3 us -> none  [the longest x3 9.69 us: pack(): jnp.dot(onehot.astype(jnp.float32), flattened, precision=lax.Precision.HI...]
    pallas_call x0 -> x2, Pallas kernels: none -> 11.8 us  [the longest x1 6.53 us: pack(): pl.pallas_call(functools.partial(pack_kernel, tile_count, blocks_owned, s...]
    all_to_all x2 -> x1, waiting for transfers between devices: 31.4 us -> 41.4 us  [per_device(): lax.all_to_all(tiles, 'tile', split_axis=0, concat_axis=0, tiled=True)]
    ppermute x4 -> x2, starting transfers between devices: 9.29 us -> 2.75 us  [shifted(): lax.ppermute(value, axis, [(source, source + steps) for source in range(f...]
    all_to_all x2 -> x1, starting transfers between devices: 13.3 us -> 6.93 us  [per_device(): lax.all_to_all(tiles, 'tile', split_axis=0, concat_axis=0, tiled=True)]
    reshape x3 -> x0, local copies, waits for them, and re-layouts: 5.49 us -> none  [the longest x1 2.71 us: per_device(): flattened = partial_value.reshape(pairs_here, cell_rows * flux_width)]
    ppermute x4 -> x2, waiting for transfers between devices: 0.01 us -> 4.72 us  [shifted(): lax.ppermute(value, axis, [(source, source + steps) for source in range(f...]
    gather x1 -> x0, local copies, waits for them, and re-layouts: 3.01 us -> none  [per_device(): chosen = grouped[pair_patch]]
  transfers between devices with their start and end apart: 6 -> 3, of which waited for: 1 -> 2; matrix products, arithmetic and copies ran while one was open for 26% -> 0% of each run, Pallas kernels for 0% -> 0%
where the time goes in v1:
time: 71.4 us; the launch traced here: 70.9 us
  waiting for transfers between devices  46.1 us (65%)
  Pallas kernels  11.8 us (17%)
  starting transfers between devices  9.68 us (14%)
  local copies, waits for them, and re-layouts  1.95 us (3%)
  between operations  0.72 us (1%)
    all_to_all x1, waiting for transfers between devices, per_device(): lax.all_to_all(tiles, 'tile', split_axis=0, concat_axis=0, tiled=True)  41.4 us
    all_to_all x1, starting transfers between devices, per_device(): lax.all_to_all(tiles, 'tile', split_axis=0, concat_axis=0, tiled=True)  6.93 us
    pallas_call x1, Pallas kernels, pack(): pl.pallas_call(functools.partial(pack_kernel, tile_count, blocks_owned, s...  6.53 us
    pallas_call x1, Pallas kernels, unpack(): pl.pallas_call(functools.partial(unpack_kernel, slots, cell_rows), out_sh...  5.29 us
    ppermute x2, waiting for transfers between devices, shifted(): lax.ppermute(value, axis, [(source, source + steps) for source in range(f...  4.72 us
    ppermute x2, starting transfers between devices, shifted(): lax.ppermute(value, axis, [(source, source + steps) for source in range(f...  2.75 us
  transfers between devices with their start and end apart: 3, of which 2 were waited for; matrix products, arithmetic and copies ran while one was open for 0% of the time, Pallas kernels for 0%

profile of v1, /device:TPU:0, one launch (start us, length us, event | category | flops | bytes accessed | tf_op | source)
XLA Modules:
  0.0 70.9 jit_solution(15750047936315162394)
XLA Ops:
  0.7 0.6 pad_add_fusion.place_ref
  1.2 0.6 broadcast_in_dim.3.empty_ref
  1.8 6.5 %pack.1 = (f32[8,520,128]{2,1,0:T(8,128)}, f32[520,128]{1,0:T(8,128)}, f32[520,128]{1,0:T(8,128)}) custom-call(s32[2]{0:T(128)} %pad_add_fusion.place_ref, s32[1]{0:T(128)S(6)} %copy.6.count_ref, s32[128]{0:T(128)} %patch_ref.1, s32[128]{0:T(128)} %atm_ref.1, s32[1408]{0:T(1024)} %broadcast_in_dim.3.empty_ref, bf16[8192,128]{1,0:T(8,128)(2,1)} %patches_hbm.1, ...), custom_call_target="tpu_custom_call" | custom-call | tf_op jit(solution)/shard_map/pack/pallas_call | solution.py:135
  8.4 0.0 copy-start.4
  8.4 0.0 copy-start.3
  8.4 6.9 %all-to-all-start = ((f32[8,520,128]{2,1,0:T(8,128)}), f32[8,520,128]{2,1,0:T(8,128)S(1)}, u32[]{:S(2)}, u32[]{:S(2)}) async-start(f32[8,520,128]{2,1,0:T(8,128)} %get-tuple-element.8), calls=%async_computation | async-start | bytes 4259840 | tf_op jit(solution)/shard_map/all_to_all | solution.py:240
  15.3 0.0 copy-done.4
  15.3 1.5 %collective-permute-start = (f32[520,128]{1,0:T(8,128)S(1)}, f32[520,128]{1,0:T(8,128)S(1)}, u32[]{:S(2)}, u32[]{:S(2)}) collective-permute-start(f32[520,128]{1,0:T(8,128)S(1)} %copy-done.4), channel_id=1, source_target_pairs={{0,8},{8,16},{16,24},{1,9},{9,17},{17,25},{2,10},{10,18},{18,26},{... | collective-permute-start | bytes 798728 | tf_op jit(solution)/shard_map/ppermute | solution.py:21
  16.8 0.0 copy-done.3
  16.8 1.3 %collective-permute-start.1 = (f32[520,128]{1,0:T(8,128)S(1)}, f32[520,128]{1,0:T(8,128)S(1)}, u32[]{:S(2)}, u32[]{:S(2)}) collective-permute-start(f32[520,128]{1,0:T(8,128)S(1)} %copy-done.3), channel_id=1, source_target_pairs={{8,0},{16,8},{24,16},{9,1},{17,9},{25,17},{10,2},{18,10},{26,18},{... | collective-permute-start | bytes 798728 | tf_op jit(solution)/shard_map/ppermute | solution.py:21
  18.1 0.0 collective-permute-done.below_hbm
  18.1 0.0 copy-start.1
  18.1 4.7 %collective-permute-done.1.above_hbm = f32[520,128]{1,0:T(8,128)S(1)} collective-permute-done((f32[520,128]{1,0:T(8,128)S(1)}, f32[520,128]{1,0:T(8,128)S(1)}, u32[]{:S(2)}, u32[]{:S(2)}) %collective-permute-start.1) | collective-permute-done | bytes 266272 | tf_op jit(solution)/shard_map/ppermute | solution.py:21
  22.8 0.0 copy-start.2
  22.8 41.4 %all-to-all-done.tile_hbm = f32[8,520,128]{2,1,0:T(8,128)S(1)} async-done(((f32[8,520,128]{2,1,0:T(8,128)}), f32[8,520,128]{2,1,0:T(8,128)S(1)}, u32[]{:S(2)}, u32[]{:S(2)}) %all-to-all-start) | async-done | bytes 2129952 | tf_op jit(solution)/shard_map/all_to_all | solution.py:240
  64.2 0.0 copy-done.1
  64.2 0.0 copy-done.2
  64.2 0.0 copy-start
  64.2 1.3 %copy-done = f32[8,520,128]{2,1,0:T(8,128)} copy-done((f32[8,520,128]{2,1,0:T(8,128)}, f32[8,520,128]{2,1,0:T(8,128)S(1)}, u32[]{:S(2)}) %copy-start) | copy-done | bytes 2129944
  65.6 5.3 %unpack.1 = f32[4096,128]{1,0:T(8,128)} custom-call(f32[8,520,128]{2,1,0:T(8,128)} %copy-done, f32[520,128]{1,0:T(8,128)} %copy-done.1, f32[520,128]{1,0:T(8,128)} %copy-done.2), custom_call_target="tpu_custom_call" | custom-call | tf_op jit(solution)/shard_map/unpack/pallas_call | solution.py:212
Async XLA Ops:
  8.4 7.0 %copy-start.4 = (f32[520,128]{1,0:T(8,128)S(1)}, f32[520,128]{1,0:T(8,128)}, u32[]{:S(2)}) copy-start(f32[520,128]{1,0:T(8,128)} %get-tuple-element.9) | copy-start | bytes 798724
  8.4 8.4 %copy-start.3 = (f32[520,128]{1,0:T(8,128)S(1)}, f32[520,128]{1,0:T(8,128)}, u32[]{:S(2)}) copy-start(f32[520,128]{1,0:T(8,128)} %get-tuple-element.10) | copy-start | bytes 798724
  8.4 55.9 %all-to-all-start = ((f32[8,520,128]{2,1,0:T(8,128)}), f32[8,520,128]{2,1,0:T(8,128)S(1)}, u32[]{:S(2)}, u32[]{:S(2)}) async-start(f32[8,520,128]{2,1,0:T(8,128)} %get-tuple-element.8), calls=%async_computation | async-start | bytes 4259840 | tf_op jit(solution)/shard_map/all_to_all | solution.py:240
  15.3 2.8 %collective-permute-start = (f32[520,128]{1,0:T(8,128)S(1)}, f32[520,128]{1,0:T(8,128)S(1)}, u32[]{:S(2)}, u32[]{:S(2)}) collective-permute-start(f32[520,128]{1,0:T(8,128)S(1)} %copy-done.4), channel_id=1, source_target_pairs={{0,8},{8,16},{16,24},{1,9},{9,17},{17,25},{2,10},{10,18},{18,26},{... | collective-permute-start | bytes 798728 | tf_op jit(solution)/shard_map/ppermute | solution.py:21
  16.8 6.0 %collective-permute-start.1 = (f32[520,128]{1,0:T(8,128)S(1)}, f32[520,128]{1,0:T(8,128)S(1)}, u32[]{:S(2)}, u32[]{:S(2)}) collective-permute-start(f32[520,128]{1,0:T(8,128)S(1)} %copy-done.3), channel_id=1, source_target_pairs={{8,0},{16,8},{24,16},{9,1},{17,9},{25,17},{10,2},{18,10},{26,18},{... | collective-permute-start | bytes 798728 | tf_op jit(solution)/shard_map/ppermute | solution.py:21
  18.1 46.1 %copy-start.1 = (f32[520,128]{1,0:T(8,128)}, f32[520,128]{1,0:T(8,128)S(1)}, u32[]{:S(2)}) copy-start(f32[520,128]{1,0:T(8,128)S(1)} %collective-permute-done.below_hbm) | copy-start | bytes 798724
  22.8 41.4 %copy-start.2 = (f32[520,128]{1,0:T(8,128)}, f32[520,128]{1,0:T(8,128)S(1)}, u32[]{:S(2)}) copy-start(f32[520,128]{1,0:T(8,128)S(1)} %collective-permute-done.1.above_hbm) | copy-start | bytes 798724
  64.2 1.3 %copy-start = (f32[8,520,128]{2,1,0:T(8,128)}, f32[8,520,128]{2,1,0:T(8,128)S(1)}, u32[]{:S(2)}) copy-start(f32[8,520,128]{2,1,0:T(8,128)S(1)} %all-to-all-done.tile_hbm) | copy-start | bytes 6389764

commit v2 on v1

v2 whole, which is shorter than its diff:
```python
import functools

import jax
import jax.numpy as jnp
from jax import lax
from jax.experimental import pallas as pl
from jax.experimental.pallas import tpu as pltpu
from jax.sharding import PartitionSpec as P

CELLS_DEV = 4096


SCALE = 2.0 ** (-27)
LABEL_ROWS = 8
UNROLL = 16
VMEM_BYTES = 16 * 2**20
PACK_VMEM = 60 * 1024 * 1024


def shifted(value, axis, steps):
    count = lax.axis_size(axis)
    first, last = (max(0, -steps), min(count, count - steps))
    return lax.ppermute(value, axis, [(source, source + steps) for source in range(first, last)])


def pack_kernel(
    tile_count, blocks_owned, slots, count_hbm, patch_hbm, atm_hbm, patches_hbm, numer_hbm, *rest
):
    outs, rest = rest[: tile_count + 2], rest[tile_count + 2 :]
    count_ref, patch_ref, atm_ref = rest[:3]
    buckets, patches, numer, table, used, row_of, patch_sem, numer_sem, index_sem = rest[3:]
    pairs_here, cell_rows, patch_rows = numer.shape
    chunks = pairs_here // UNROLL
    flux_width = buckets.shape[2]
    bucket_rows = slots * cell_rows + LABEL_ROWS
    index_copies = [
        pltpu.make_async_copy(count_hbm, count_ref, index_sem.at[0]),
        pltpu.make_async_copy(patch_hbm, patch_ref, index_sem.at[1]),
        pltpu.make_async_copy(atm_hbm, atm_ref, index_sem.at[2]),
    ]
    for copy in index_copies:
        copy.start()
    patch_copy = pltpu.make_async_copy(patches_hbm, patches, patch_sem)
    patch_copy.start()

    def numer_copy(chunk):
        part = pl.ds(pl.multiple_of(chunk * UNROLL, UNROLL), UNROLL)
        return pltpu.make_async_copy(numer_hbm.at[part], numer.at[part], numer_sem.at[chunk])

    for chunk in range(chunks):
        numer_copy(chunk).start()

    band_now, tile_now = lax.axis_index("band"), lax.axis_index("tile")

    def clear(step, carry):
        rows = pl.ds(pl.multiple_of(step * cell_rows, cell_rows), cell_rows)
        for bucket in range(tile_count + 2):
            buckets[bucket, rows, :] = jnp.zeros((cell_rows, flux_width), jnp.float32)
        return carry

    lax.fori_loop(0, slots, clear, 0)

    def forget(step, carry):
        for inner in range(16):
            table[step * 16 + inner] = -1
        return carry

    lax.fori_loop(0, (tile_count + 3) * blocks_owned // 16, forget, 0)
    for bucket in range(tile_count + 2):
        buckets[bucket, pl.ds(slots * cell_rows, LABEL_ROWS), :] = jnp.zeros((LABEL_ROWS, flux_width), jnp.float32)
        used[bucket] = 0
    used[tile_count + 2] = 0
    lane = lax.broadcasted_iota(jnp.int32, (1, flux_width), 1)
    for copy in index_copies:
        copy.wait()
    count = count_ref[0]

    def place(step, carry):
        for inner in range(4):
            pair = step * 4 + inner
            live = pair < count
            atm = atm_ref[pair]
            owner = lax.div(atm, blocks_owned)
            block = atm - owner * blocks_owned
            owner_band = lax.div(owner, tile_count)
            owner_tile = owner - owner_band * tile_count
            beyond = jnp.where(owner_band > band_now, tile_count, tile_count + 1)
            bucket = jnp.where(owner_band == band_now, owner_tile ^ tile_now, beyond)
            bucket = jnp.where(live, bucket, tile_count + 2)
            key = bucket * blocks_owned + block
            known = table[key]
            fresh = known < 0
            slot = jnp.where(fresh, used[bucket], known)
            slot = jnp.where(live, slot, 0)
            table[key] = slot
            used[bucket] = used[bucket] + jnp.where(fresh, 1, 0)
            row_of[pair] = bucket * bucket_rows + slot * cell_rows
            row = pl.ds(slots * cell_rows, 1)
            label = (block + 1).astype(jnp.float32)
            buckets[bucket, row, :] = jnp.where(lane == slot, label, buckets[bucket, row, :])
        return carry

    lax.fori_loop(0, pairs_here // 4, place, 0)
    patch_copy.wait()
    flat = buckets.reshape(buckets.shape[0] * bucket_rows, flux_width)

    def multiply(chunk, carry):
        numer_copy(chunk).wait()
        results = []
        for inner in range(UNROLL):
            pair = chunk * UNROLL + inner
            weight = (numer[pair].astype(jnp.float32) * SCALE).astype(jnp.bfloat16)
            start = pl.multiple_of(patch_ref[pair] * patch_rows, patch_rows)
            source = patches[pl.ds(start, patch_rows), :]
            results.append(jnp.dot(weight, source, preferred_element_type=jnp.float32))
        for inner in range(UNROLL):
            rows = pl.ds(pl.multiple_of(row_of[chunk * UNROLL + inner], 8), cell_rows)
            flat[rows, :] = flat[rows, :] + results[inner]
        return carry

    busy = lax.div(count + UNROLL - 1, UNROLL)
    lax.fori_loop(0, busy, multiply, 0)

    def drain(chunk, carry):
        numer_copy(chunk).wait()
        return carry

    lax.fori_loop(busy, chunks, drain, 0)

    def hand_over(step, carry):
        rows = pl.ds(pl.multiple_of(step * cell_rows, cell_rows), cell_rows)
        for bucket, out in enumerate(outs):
            out[rows, :] = buckets[bucket, rows, :]
        return carry

    lax.fori_loop(0, slots, hand_over, 0)
    rows = pl.ds(slots * cell_rows, LABEL_ROWS)
    for bucket, out in enumerate(outs):
        out[rows, :] = buckets[bucket, rows, :]


def pack(counts, pair_patch, pair_atm, patches, numer, tile_count, blocks_owned, slots):
    pairs_here, cell_rows, patch_rows = numer.shape
    flux_width = patches.shape[1]
    bucket_rows = slots * cell_rows + LABEL_ROWS
    keys = (tile_count + 3) * blocks_owned
    hbm, vmem = pl.BlockSpec(memory_space=pltpu.HBM), pl.BlockSpec(memory_space=pltpu.VMEM)
    bucket = jax.ShapeDtypeStruct((bucket_rows, flux_width), jnp.float32)
    return pl.pallas_call(
        functools.partial(pack_kernel, tile_count, blocks_owned, slots),
        out_shape=(bucket,) * (tile_count + 2),
        in_specs=[hbm] * 5,
        out_specs=(vmem,) * (tile_count + 2),
        scratch_shapes=[
            pltpu.SMEM(counts.shape, jnp.int32),
            pltpu.SMEM((pairs_here,), jnp.int32),
            pltpu.SMEM((pairs_here,), jnp.int32),
            pltpu.VMEM((tile_count + 3, bucket_rows, flux_width), jnp.float32),
            pltpu.VMEM(patches.shape, patches.dtype),
            pltpu.VMEM(numer.shape, numer.dtype),
            pltpu.SMEM((keys,), jnp.int32),
            pltpu.SMEM((tile_count + 3,), jnp.int32),
            pltpu.SMEM((pairs_here,), jnp.int32),
            pltpu.SemaphoreType.DMA,
            pltpu.SemaphoreType.DMA((pairs_here // UNROLL,)),
            pltpu.SemaphoreType.DMA((3,)),
        ],
        compiler_params=pltpu.CompilerParams(vmem_limit_bytes=PACK_VMEM),
        name="pack",
    )(counts, pair_patch, pair_atm, patches, numer)


def add_parts(parts, total, label_rows, labels, label_sem, slots, cell_rows):
    for index, part in enumerate(parts):
        row = part[pl.ds(slots * cell_rows, 1), :]
        label_rows[pl.ds(index, 1), :] = row.astype(jnp.int32) - 1
    label_copy = pltpu.make_async_copy(label_rows, labels, label_sem)
    label_copy.start()
    label_copy.wait()
    for index, part in enumerate(parts):
        def add(slot, carry):
            label = labels[index, slot]

            @pl.when(label >= 0)
            def _():
                rows = pl.ds(pl.multiple_of(label * cell_rows, cell_rows), cell_rows)
                here = pl.ds(pl.multiple_of(slot * cell_rows, cell_rows), cell_rows)
                total[rows, :] = total[rows, :] + part[here, :]

            return carry

        lax.fori_loop(0, slots, add, 0)


def first_kernel(count, slots, cell_rows, *rest):
    parts, (total, label_rows, labels, label_sem) = rest[:count], rest[count:]

    def clear(step, carry):
        rows = pl.ds(pl.multiple_of(step * 128, 128), 128)
        total[rows, :] = jnp.zeros((128, total.shape[1]), jnp.float32)
        return carry

    lax.fori_loop(0, total.shape[0] // 128, clear, 0)
    add_parts(parts, total, label_rows, labels, label_sem, slots, cell_rows)


def last_kernel(count, slots, cell_rows, *rest):
    parts, (before, total, out_hbm, label_rows, labels, label_sem, out_sem) = rest[:count], rest[count:]
    del before
    add_parts(parts, total, label_rows, labels, label_sem, slots, cell_rows)
    out_copy = pltpu.make_async_copy(total, out_hbm, out_sem)
    out_copy.start()
    out_copy.wait()


def unpack(parts, before, blocks_owned, cell_rows, slots):
    flux_width = parts[0].shape[1]
    hbm, vmem = pl.BlockSpec(memory_space=pl.ANY), pl.BlockSpec(memory_space=pltpu.VMEM)
    total = jax.ShapeDtypeStruct((blocks_owned * cell_rows, flux_width), jnp.float32)
    label_shape = (-(-len(parts) // 8) * 8, flux_width)
    scratch = [
        pltpu.VMEM(label_shape, jnp.int32),
        pltpu.SMEM(label_shape, jnp.int32),
        pltpu.SemaphoreType.DMA,
    ]
    params = pltpu.CompilerParams(vmem_limit_bytes=VMEM_BYTES)
    if before is None:
        return pl.pallas_call(
            functools.partial(first_kernel, len(parts), slots, cell_rows),
            out_shape=total,
            in_specs=[vmem] * len(parts),
            out_specs=vmem,
            scratch_shapes=scratch,
            compiler_params=params,
            name="unpack_first",
        )(*parts)
    return pl.pallas_call(
        functools.partial(last_kernel, len(parts), slots, cell_rows),
        out_shape=(total, total),
        in_specs=[vmem] * (len(parts) + 1),
        out_specs=(vmem, hbm),
        scratch_shapes=scratch + [pltpu.SemaphoreType.DMA],
        input_output_aliases={len(parts): 0},
        compiler_params=params,
        name="unpack_last",
    )(*parts, before)[1]


def per_device(patches, pair_patch, pair_atm, numerators, counts):
    pairs_here, patch_rows, cell_rows = numerators.shape
    blocks_owned = CELLS_DEV // cell_rows
    slots = pairs_here // 8
    tile_count = lax.axis_size("tile")
    numer = jnp.swapaxes(numerators, 1, 2)
    own, *parts = pack(counts, pair_patch, pair_atm, patches, numer, tile_count, blocks_owned, slots)
    received = {}
    for mask in reversed(range(1, tile_count)):
        pairs = [(tile, tile ^ mask) for tile in range(tile_count)]
        received[mask] = lax.ppermute(parts[mask - 1], "tile", pairs)
    bands = [shifted(parts[tile_count - 1], "band", 1), shifted(parts[tile_count], "band", -1)]
    half = tile_count // 2
    early = [own, *bands] + [received[mask] for mask in range(1, half)]
    total = unpack(early, None, blocks_owned, cell_rows, slots)
    late = [received[mask] for mask in range(half, tile_count)]
    return unpack(late, total, blocks_owned, cell_rows, slots)


def solution(mesh):
    placed = (
        P(("band", "tile"), None),
        P(("band", "tile")),
        P(("band", "tile")),
        P(("band", "tile"), None, None),
        P(("band", "tile")),
    )
    return jax.shard_map(
        per_device, mesh=mesh, in_specs=placed, out_specs=P(("band", "tile"), None), check_vma=False
    )
```

time: 71.4 us -> 66.5 us (0.931)
  the two profiles are of different devices: /device:TPU:0 before, /device:TPU:11 now
where the time goes in v2:
time: 66.5 us; the launch traced here: 66.3 us
  waiting for transfers between devices  38.2 us (57%)
  starting transfers between devices  13.9 us (21%)
  Pallas kernels  12.5 us (19%)
  local copies, waits for them, and re-layouts  0.95 us (1%)
  between operations  0.72 us (1%)
    ppermute x7, waiting for transfers between devices, per_device(): received[mask] = lax.ppermute(parts[mask - 1], 'tile', pairs)  36.2 us
    ppermute x7, starting transfers between devices, per_device(): received[mask] = lax.ppermute(parts[mask - 1], 'tile', pairs)  8.55 us
    pallas_call x1, Pallas kernels, pack(): pl.pallas_call(functools.partial(pack_kernel, tile_count, blocks_owned, s...  7.19 us
    ppermute x2, starting transfers between devices, shifted(): lax.ppermute(value, axis, [(source, source + steps) for source in range(f...  5.37 us
    pallas_call x1, Pallas kernels, unpack(): pl.pallas_call(functools.partial(last_kernel, len(parts), slots, cell_row...  2.94 us
    pallas_call x1, Pallas kernels, unpack(): pl.pallas_call(functools.partial(first_kernel, len(parts), slots, cell_ro...  2.33 us
    ppermute x2, waiting for transfers between devices, shifted(): lax.ppermute(value, axis, [(source, source + steps) for source in range(f...  2.05 us
  transfers between devices with their start and end apart: 9, of which 7 were waited for; matrix products, arithmetic and copies ran while one was open for 0% of the time, Pallas kernels for 4%

profile of v2, /device:TPU:11, one launch (start us, length us, event | category | flops | bytes accessed | tf_op | source)
XLA Modules:
  0.0 66.3 jit_solution(17500024516399039834)
XLA Ops:
  0.7 7.2 %pack.1 = (f32[520,128]{1,0:T(8,128)}, f32[520,128]{1,0:T(8,128)}, f32[520,128]{1,0:T(8,128)}, f32[520,128]{1,0:T(8,128)}, f32[520,128]{1,0:T(8,128)}, /*index=5...) custom-call(s32[1]{0:T(128)S(6)} %copy.8.count_hbm, ...), custom_call_target="tpu_custom_call" | custom-call | tf_op jit(solution)/shard_map/pack/pallas_call | solution.py:149
  7.9 3.5 %collective-permute-start.4 = (f32[520,128]{1,0:T(8,128)}, f32[520,128]{1,0:T(8,128)S(1)}, u32[]{:S(2)}, u32[]{:S(2)}) collective-permute-start(f32[520,128]{1,0:T(8,128)} %get-tuple-element.21), channel_id=1, source_target_pairs={{0,8},{8,16},{16,24},{1,9},{9,17},{17,25},{2,10},{10,18},{18,26},{... | collective-permute-start | bytes 798728 | tf_op jit(solution)/shard_map/ppermute | solution.py:23
  11.3 1.9 %collective-permute-start.5 = (f32[520,128]{1,0:T(8,128)}, f32[520,128]{1,0:T(8,128)S(1)}, u32[]{:S(2)}, u32[]{:S(2)}) collective-permute-start(f32[520,128]{1,0:T(8,128)} %get-tuple-element.22), channel_id=1, source_target_pairs={{8,0},{16,8},{24,16},{9,1},{17,9},{25,17},{10,2},{18,10},{26,18},{... | collective-permute-start | bytes 798728 | tf_op jit(solution)/shard_map/ppermute | solution.py:23
  13.2 0.1 collective-permute-start.6
  13.3 0.1 collective-permute-start.7
  13.4 2.7 %collective-permute-start = (f32[520,128]{1,0:T(8,128)}, f32[520,128]{1,0:T(8,128)S(1)}, u32[]{:S(2)}, u32[]{:S(2)}) collective-permute-start(f32[520,128]{1,0:T(8,128)} %get-tuple-element.16), channel_id=1, source_target_pairs={{0,4},{1,5},{2,6},{3,7},{4,0},{5,1},{6,2},{7,3},{8,12},{9,13},{10,... | collective-permute-start | bytes 798728 | tf_op jit(solution)/shard_map/ppermute | solution.py:259
  16.1 0.0 collective-permute-done.4.rest_1_
  16.1 1.4 %collective-permute-start.1 = (f32[520,128]{1,0:T(8,128)}, f32[520,128]{1,0:T(8,128)S(1)}, u32[]{:S(2)}, u32[]{:S(2)}) collective-permute-start(f32[520,128]{1,0:T(8,128)} %get-tuple-element.17), channel_id=1, source_target_pairs={{0,5},{1,4},{2,7},{3,6},{4,1},{5,0},{6,3},{7,2},{8,13},{9,12},{10,... | collective-permute-start | bytes 798728 | tf_op jit(solution)/shard_map/ppermute | solution.py:259
  17.5 2.0 %collective-permute-done.5.rest_2_ = f32[520,128]{1,0:T(8,128)S(1)} collective-permute-done((f32[520,128]{1,0:T(8,128)}, f32[520,128]{1,0:T(8,128)S(1)}, u32[]{:S(2)}, u32[]{:S(2)}) %collective-permute-start.5) | collective-permute-done | bytes 266272 | tf_op jit(solution)/shard_map/ppermute | solution.py:23
  19.6 0.0 collective-permute-start.8
  19.6 0.9 %collective-permute-done.6.rest_3_ = f32[520,128]{1,0:T(8,128)S(1)} collective-permute-done((f32[520,128]{1,0:T(8,128)}, f32[520,128]{1,0:T(8,128)S(1)}, u32[]{:S(2)}, u32[]{:S(2)}) %collective-permute-start.6) | collective-permute-done | bytes 266272 | tf_op jit(solution)/shard_map/ppermute | solution.py:259
  20.4 1.9 %collective-permute-start.2 = (f32[520,128]{1,0:T(8,128)}, f32[520,128]{1,0:T(8,128)S(1)}, u32[]{:S(2)}, u32[]{:S(2)}) collective-permute-start(f32[520,128]{1,0:T(8,128)} %get-tuple-element.18), channel_id=1, source_target_pairs={{0,6},{1,7},{2,4},{3,5},{4,2},{5,3},{6,0},{7,1},{8,14},{9,15},{10,... | collective-permute-start | bytes 798728 | tf_op jit(solution)/shard_map/ppermute | solution.py:259
  22.4 3.0 %collective-permute-done.7.rest_4_ = f32[520,128]{1,0:T(8,128)S(1)} collective-permute-done((f32[520,128]{1,0:T(8,128)}, f32[520,128]{1,0:T(8,128)S(1)}, u32[]{:S(2)}, u32[]{:S(2)}) %collective-permute-start.7) | collective-permute-done | bytes 266272 | tf_op jit(solution)/shard_map/ppermute | solution.py:259
  25.4 2.4 %collective-permute-start.3 = (f32[520,128]{1,0:T(8,128)}, f32[520,128]{1,0:T(8,128)S(1)}, u32[]{:S(2)}, u32[]{:S(2)}) collective-permute-start(f32[520,128]{1,0:T(8,128)} %get-tuple-element.19), channel_id=1, source_target_pairs={{0,7},{1,6},{2,5},{3,4},{4,3},{5,2},{6,1},{7,0},{8,15},{9,14},{10,... | collective-permute-start | bytes 798728 | tf_op jit(solution)/shard_map/ppermute | solution.py:259
  27.8 12.7 %collective-permute-done.8.rest_5_ = f32[520,128]{1,0:T(8,128)S(1)} collective-permute-done((f32[520,128]{1,0:T(8,128)}, f32[520,128]{1,0:T(8,128)S(1)}, u32[]{:S(2)}, u32[]{:S(2)}) %collective-permute-start.8) | collective-permute-done | bytes 266272 | tf_op jit(solution)/shard_map/ppermute | solution.py:259
  40.5 0.0 copy-start
  40.5 0.9 %copy-done = f32[520,128]{1,0:T(8,128)S(1)} copy-done((f32[520,128]{1,0:T(8,128)S(1)}, f32[520,128]{1,0:T(8,128)}, u32[]{:S(2)}) %copy-start) | copy-done | bytes 266264
  41.4 2.3 %unpack_first.1.rest_4_ = f32[4096,128]{1,0:T(8,128)S(1)} custom-call(f32[520,128]{1,0:T(8,128)S(1)} %copy-done, f32[520,128]{1,0:T(8,128)S(1)} %collective-permute-done.4.rest_1_, f32[520,128]{1,0:T(8,128)S(1)} %collective-permute-done.5.rest_2_, f32[520,128]{1,0:T(8,128)S(1)} %collective-permute-done.6.rest_3_, ...), custom_call_target="tpu_custom_call" | custom-call | tf_op jit(solution)/shard_map/unpack_first/pallas_call | solution.py:228
  43.8 0.0 collective-permute-done.rest_0_
  43.8 7.4 %collective-permute-done.1.rest_1_ = f32[520,128]{1,0:T(8,128)S(1)} collective-permute-done((f32[520,128]{1,0:T(8,128)}, f32[520,128]{1,0:T(8,128)S(1)}, u32[]{:S(2)}, u32[]{:S(2)}) %collective-permute-start.1) | collective-permute-done | bytes 266272 | tf_op jit(solution)/shard_map/ppermute | solution.py:259
  51.2 6.6 %collective-permute-done.2.rest_2_ = f32[520,128]{1,0:T(8,128)S(1)} collective-permute-done((f32[520,128]{1,0:T(8,128)}, f32[520,128]{1,0:T(8,128)S(1)}, u32[]{:S(2)}, u32[]{:S(2)}) %collective-permute-start.2) | collective-permute-done | bytes 266272 | tf_op jit(solution)/shard_map/ppermute | solution.py:259
  57.8 5.5 %collective-permute-done.3.rest_3_ = f32[520,128]{1,0:T(8,128)S(1)} collective-permute-done((f32[520,128]{1,0:T(8,128)}, f32[520,128]{1,0:T(8,128)S(1)}, u32[]{:S(2)}, u32[]{:S(2)}) %collective-permute-start.3) | collective-permute-done | bytes 266272 | tf_op jit(solution)/shard_map/ppermute | solution.py:259
  63.4 2.9 %unpack_last.1 = (f32[4096,128]{1,0:T(8,128)S(1)}, f32[4096,128]{1,0:T(8,128)}) custom-call(f32[520,128]{1,0:T(8,128)S(1)} %collective-permute-done.rest_0_, f32[520,128]{1,0:T(8,128)S(1)} %collective-permute-done.1.rest_1_, f32[520,128]{1,0:T(8,128)S(1)} %collective-permute-done.2.rest_2_, ...), custom_call_target="tpu_custom_call", output_to_operand_aliasing={{0}: (4, {})} | custom-call | tf_op jit(solution)/shard_map/unpack_last/pallas_call | solution.py:237
Async XLA Ops:
  7.9 8.3 %collective-permute-start.4 = (f32[520,128]{1,0:T(8,128)}, f32[520,128]{1,0:T(8,128)S(1)}, u32[]{:S(2)}, u32[]{:S(2)}) collective-permute-start(f32[520,128]{1,0:T(8,128)} %get-tuple-element.21), channel_id=1, source_target_pairs={{0,8},{8,16},{16,24},{1,9},{9,17},{17,25},{2,10},{10,18},{18,26},{... | collective-permute-start | bytes 798728 | tf_op jit(solution)/shard_map/ppermute | solution.py:23
  11.3 8.2 %collective-permute-start.5 = (f32[520,128]{1,0:T(8,128)}, f32[520,128]{1,0:T(8,128)S(1)}, u32[]{:S(2)}, u32[]{:S(2)}) collective-permute-start(f32[520,128]{1,0:T(8,128)} %get-tuple-element.22), channel_id=1, source_target_pairs={{8,0},{16,8},{24,16},{9,1},{17,9},{25,17},{10,2},{18,10},{26,18},{... | collective-permute-start | bytes 798728 | tf_op jit(solution)/shard_map/ppermute | solution.py:23
  13.2 7.2 %collective-permute-start.6 = (f32[520,128]{1,0:T(8,128)}, f32[520,128]{1,0:T(8,128)S(1)}, u32[]{:S(2)}, u32[]{:S(2)}) collective-permute-start(f32[520,128]{1,0:T(8,128)} %get-tuple-element.23), channel_id=1, source_target_pairs={{0,1},{1,0},{2,3},{3,2},{4,5},{5,4},{6,7},{7,6},{8,9},{9,8},{10,11... | collective-permute-start | bytes 798728 | tf_op jit(solution)/shard_map/ppermute | solution.py:259
  13.3 12.1 %collective-permute-start.7 = (f32[520,128]{1,0:T(8,128)}, f32[520,128]{1,0:T(8,128)S(1)}, u32[]{:S(2)}, u32[]{:S(2)}) collective-permute-start(f32[520,128]{1,0:T(8,128)} %get-tuple-element.24), channel_id=1, source_target_pairs={{0,2},{1,3},{2,0},{3,1},{4,6},{5,7},{6,4},{7,5},{8,10},{9,11},{10,... | collective-permute-start | bytes 798728 | tf_op jit(solution)/shard_map/ppermute | solution.py:259
  13.4 30.4 %collective-permute-start = (f32[520,128]{1,0:T(8,128)}, f32[520,128]{1,0:T(8,128)S(1)}, u32[]{:S(2)}, u32[]{:S(2)}) collective-permute-start(f32[520,128]{1,0:T(8,128)} %get-tuple-element.16), channel_id=1, source_target_pairs={{0,4},{1,5},{2,6},{3,7},{4,0},{5,1},{6,2},{7,3},{8,12},{9,13},{10,... | collective-permute-start | bytes 798728 | tf_op jit(solution)/shard_map/ppermute | solution.py:259
  16.1 35.1 %collective-permute-start.1 = (f32[520,128]{1,0:T(8,128)}, f32[520,128]{1,0:T(8,128)S(1)}, u32[]{:S(2)}, u32[]{:S(2)}) collective-permute-start(f32[520,128]{1,0:T(8,128)} %get-tuple-element.17), channel_id=1, source_target_pairs={{0,5},{1,4},{2,7},{3,6},{4,1},{5,0},{6,3},{7,2},{8,13},{9,12},{10,... | collective-permute-start | bytes 798728 | tf_op jit(solution)/shard_map/ppermute | solution.py:259
  19.6 20.9 %collective-permute-start.8 = (f32[520,128]{1,0:T(8,128)}, f32[520,128]{1,0:T(8,128)S(1)}, u32[]{:S(2)}, u32[]{:S(2)}) collective-permute-start(f32[520,128]{1,0:T(8,128)} %get-tuple-element.25), channel_id=1, source_target_pairs={{0,3},{1,2},{2,1},{3,0},{4,7},{5,6},{6,5},{7,4},{8,11},{9,10},{10,... | collective-permute-start | bytes 798728 | tf_op jit(solution)/shard_map/ppermute | solution.py:259
  20.4 37.4 %collective-permute-start.2 = (f32[520,128]{1,0:T(8,128)}, f32[520,128]{1,0:T(8,128)S(1)}, u32[]{:S(2)}, u32[]{:S(2)}) collective-permute-start(f32[520,128]{1,0:T(8,128)} %get-tuple-element.18), channel_id=1, source_target_pairs={{0,6},{1,7},{2,4},{3,5},{4,2},{5,3},{6,0},{7,1},{8,14},{9,15},{10,... | collective-permute-start | bytes 798728 | tf_op jit(solution)/shard_map/ppermute | solution.py:259
  25.4 37.9 %collective-permute-start.3 = (f32[520,128]{1,0:T(8,128)}, f32[520,128]{1,0:T(8,128)S(1)}, u32[]{:S(2)}, u32[]{:S(2)}) collective-permute-start(f32[520,128]{1,0:T(8,128)} %get-tuple-element.19), channel_id=1, source_target_pairs={{0,7},{1,6},{2,5},{3,4},{4,3},{5,2},{6,1},{7,0},{8,15},{9,14},{10,... | collective-permute-start | bytes 798728 | tf_op jit(solution)/shard_map/ppermute | solution.py:259
  40.5 1.0 %copy-start = (f32[520,128]{1,0:T(8,128)S(1)}, f32[520,128]{1,0:T(8,128)}, u32[]{:S(2)}) copy-start(f32[520,128]{1,0:T(8,128)} %get-tuple-element.20.rest_0_) | copy-start | bytes 798724
